TPU v7x, 32 devices: a whole 2x2x4 slice. The times are simulated.
32 devices in a mesh: px: 2 (over core), py: 4 (over z), ta: 4 (over y, x).
Axes of the slice: x: 2, y: 2, z: 4, core: 2. Of those that a mesh axis runs over, the one named last changes fastest.
Arguments:
- snapshots: bfloat16 [384, 5, 65536], P('ta', None, ('px', 'py')), may hold values from -6 to 6
- quad_weights: float32 [65536], P(('px', 'py')), may hold values from 1 to 10
- spectral_indices: int32 [32], replicated, may hold values from 0 to 127
Outputs:
- spectra: float32 [32, 2, 2, 5, 65536], P('ta', None, None, None, ('px', 'py'))
- gram: float32 [32, 2, 2, 2], P('ta')
All inputs are finite; a program needn't handle non-finite values.
Results may differ from a plain program's by a relative error of at most 0.0042.
Values may be sent and summed in bfloat16 or wider, within the bound.
A program may use at most 128 MiB of HBM per device.

v0:
```python
import math
import jax
import jax.numpy as jnp
from jax import lax
from jax.sharding import PartitionSpec as P

VARS = 5
BLK = 256
HOP = 128
SEGMENT_NUMBER = 2
RETAINED_MODES = 32


def make_rotation_multipliers(spectral_indices, temporal_locations):
    segment_beginnings = jnp.arange(SEGMENT_NUMBER, dtype=jnp.int32) * HOP
    segment_shifts = temporal_locations[None, :] - segment_beginnings[:, None]
    inside = (segment_shifts >= 0) & (segment_shifts < BLK)
    window = 0.5 - 0.5 * jnp.cos(2.0 * math.pi * segment_shifts.astype(jnp.float32) / BLK)
    window = jnp.where(inside, window, jnp.float32(0.0)) / jnp.sqrt(jnp.float32(3.0 * BLK / 8.0))
    phases = jnp.mod(spectral_indices[:, None, None] * segment_shifts[None, :, :], BLK)
    angles = 2.0 * math.pi * phases.astype(jnp.float32) / BLK
    real_part = jnp.cos(angles) * window[None]
    imag_part = -jnp.sin(angles) * window[None]
    gathered_segments = jnp.stack([real_part, imag_part], axis=2)
    return gathered_segments.reshape(
        RETAINED_MODES * SEGMENT_NUMBER * 2, temporal_locations.shape[0]
    ).astype(jnp.bfloat16)


def gram_terms(spectra):
    flat = spectra.reshape(spectra.shape[0], 2 * SEGMENT_NUMBER, -1)
    inner = jnp.einsum("fam,fbm->fab", flat, flat, precision=lax.Precision.HIGHEST)
    inner = inner.reshape(spectra.shape[0], SEGMENT_NUMBER, 2, SEGMENT_NUMBER, 2)
    real_part = inner[:, :, 0, :, 0] + inner[:, :, 1, :, 1]
    imag_part = inner[:, :, 0, :, 1] - inner[:, :, 1, :, 0]
    return jnp.stack([real_part, imag_part], axis=-1)


def on_device(snapshots, quad_weights, spectral_indices):
    record_length = snapshots.shape[0]
    point_count = snapshots.shape[2]
    groups = lax.axis_size("ta")
    temporal_locations = lax.axis_index("ta") * record_length + jnp.arange(
        record_length, dtype=jnp.int32
    )
    rotation_multipliers = make_rotation_multipliers(spectral_indices, temporal_locations)
    flat_snapshots = snapshots.reshape(record_length, VARS * point_count)
    raw = lax.psum_scatter(
        jnp.dot(rotation_multipliers, flat_snapshots, preferred_element_type=jnp.float32),
        "ta",
        scatter_dimension=0,
        tiled=True,
    )
    raw = raw.reshape(RETAINED_MODES // groups, SEGMENT_NUMBER, 2, VARS, point_count)
    spectra = raw * jnp.sqrt(quad_weights)
    summed = lax.psum(gram_terms(spectra), ("px", "py"))
    total_points = point_count * lax.axis_size("px") * lax.axis_size("py")
    gram = summed / jnp.float32(total_points * VARS)
    return (spectra, gram)


def solution(mesh):
    return jax.shard_map(
        on_device,
        mesh=mesh,
        in_specs=(P("ta", None, ("px", "py")), P(("px", "py")), P()),
        out_specs=(P("ta", None, None, None, ("px", "py")), P("ta", None, None, None)),
        check_vma=False,
    )
```

profile of v0, /device:TPU:1, one launch (start us, length us, event | category | flops | bytes accessed | tf_op | source)
XLA Modules:
  0.0 306.7 jit_solution(16101970219021868528)
XLA Ops:
  7.2 0.0 reduce-scatter.2.cloned.1.call-start
  7.2 0.1 broadcast_subtract_fusion
  7.3 0.1 fusion.6
  7.4 0.9 multiply_convert_fusion.1
  8.4 12.7 %copy.17 = bf16[96,5,8192]{0,2,1:T(8,128)(2,1)} copy(bf16[96,5,8192]{2,0,1:T(8,128)(2,1)} %param.3) | data formatting | bytes 15728640 | tf_op args[0]
  21.1 13.8 %fusion.7 = f32[128,40960]{1,0:T(8,128)} fusion(bf16[128,96]{1,0:T(8,128)(2,1)S(1)} %bitcast.8, bf16[96,40960]{0,1:T(8,128)(2,1)} %bitcast.7), kind=kOutput, calls=%fused_computation.24 | convolution fusion | flops 1006632960 | bytes 28860416 | tf_op jit(solution)/shard_map/dot_general | solution.py:49
  34.9 0.0 copy-start
  34.9 0.0 reduce-scatter.2.cloned.1.call-update
  35.0 0.7 copy-done
  35.7 0.1 mul.103
  35.8 188.9 %reduce-scatter.2.cloned.1.call-done = f32[32,40960]{1,0:T(8,128)} async-done(((f32[128,40960]{1,0:T(8,128)}), f32[32,40960]{1,0:T(8,128)}) %reduce-scatter.2.cloned.1.call-update) | async-done | bytes 5242896 | tf_op jit(solution)/shard_map/reduce_scatter | solution.py:48
  224.8 5.8 %reshape.194 = f32[8,4,40960]{2,1,0:T(4,128)} reshape(f32[32,40960]{1,0:T(8,128)} %reduce-scatter.2.cloned.1.call-done) | data formatting | bytes 10485760 | tf_op jit(solution)/shard_map/reshape | solution.py:54
  230.6 25.9 %fusion = f32[8,4,4]{2,1,0:T(4,128)S(1)} fusion(f32[8,4,40960]{2,1,0:T(4,128)} %reshape.194, f32[40960]{0:T(1024)S(1)} %mul.103), kind=kOutput, calls=%fused_computation | convolution fusion | flops 64225280 | bytes 5407232 | tf_op jit(solution)/shard_map/fam,fbm->fab/dot_general | solution.py:32
  256.5 0.1 copy.18
  256.7 17.6 %psum.7 = f32[8,2,2,2]{0,2,3,1:T(2,128)S(1)} all-reduce(f32[8,2,2,2]{0,2,3,1:T(2,128)S(1)} %pad_maximum_fusion.1), channel_id=1, replica_groups=mesh['px'=2,'py'=4,'ta'=4] {'px','py'}, use_global_device_ids=true, to_apply=%region_1.2 | all-reduce | flops 64 | bytes 512 | tf_op jit(solution)/shard_map/psum | solution.py:56
  274.3 0.6 copy.20
  274.9 7.3 %reshape.193 = f32[8,2,2,5,8192]{4,3,2,1,0:T(8,128)} reshape(f32[32,40960]{1,0:T(8,128)} %reduce-scatter.2.cloned.1.call-done) | data formatting | bytes 10485760 | tf_op jit(solution)/shard_map/reshape | solution.py:54
  282.2 7.8 %broadcast_multiply_fusion = f32[8,2,2,5,8192]{4,3,2,1,0:T(8,128)} fusion(f32[8,2,2,5,8192]{4,3,2,1,0:T(8,128)} %reshape.193, f32[8192]{0:T(1024)S(1)} %sqrt.3), kind=kLoop, calls=%fused_computation.2 | loop fusion | flops 1310720 | bytes 10518528 | tf_op jit(solution)/shard_map/mul | solution.py:55
  290.0 9.8 %copy.19 = f32[8,2,2,5,8192]{4,2,3,1,0:T(2,128)} copy(f32[8,2,2,5,8192]{4,3,2,1,0:T(8,128)} %broadcast_multiply_fusion) | data formatting | bytes 10485760
  (9 shorter events, 0.1 us)
Async XLA Ops:
  7.2 217.6 %reduce-scatter.2.cloned.1.call-start = ((), (), s32[]{:S(2)}) async-start(), calls=%async_computation.1 | async-start | bytes 26214400 | tf_op jit(solution)/shard_map/reduce_scatter | solution.py:48
  34.9 0.8 copy-start
Sparse Core Ops, SparseCore 0:
  35.1 189.6 reduce-scatter.1
where the time goes:
time: 308 us; the launch traced here: 307 us
  waiting for transfers between devices  189 us (61%)
  matrix products  39.8 us (13%)
  local copies, waits for them, and re-layouts  37.3 us (12%)
  blocking collectives  17.6 us (6%)
  between operations  14.1 us (5%)
  other arithmetic  8.87 us (3%)
    reduce_scatter x1, waiting for transfers between devices, on_device(): lax.psum_scatter(jnp.dot(rotation_multipliers, flat_snapshots, preferred_...  189 us
    dot_general x1, matrix products, gram_terms(): jnp.einsum('fam,fbm->fab', flat, flat, precision=lax.Precision.HIGHEST)  25.9 us
    unnamed x5, local copies, waits for them, and re-layouts  23.9 us
    psum x1, blocking collectives, on_device(): summed = lax.psum(gram_terms(spectra), ('px', 'py'))  17.6 us
    dot_general x1, matrix products, on_device(): jnp.dot(rotation_multipliers, flat_snapshots, preferred_element_type=jnp....  13.8 us
    reshape x2, local copies, waits for them, and re-layouts, on_device(): raw.reshape(RETAINED_MODES // groups, SEGMENT_NUMBER, 2, VARS, point_count)  13.2 us
    mul x1, other arithmetic, on_device(): spectra = raw * jnp.sqrt(quad_weights)  7.76 us
  transfers between devices with their start and end apart: 1, of which 1 were waited for; matrix products, arithmetic and copies ran while one was open for 0% of the time, Pallas kernels for 0%

commit v1 on v0

--- a/solution.py
+++ b/solution.py
@@ -53,7 +53,7 @@
     )
     raw = raw.reshape(RETAINED_MODES // groups, SEGMENT_NUMBER, 2, VARS, point_count)
     spectra = raw * jnp.sqrt(quad_weights)
-    summed = lax.psum(gram_terms(spectra), ("px", "py"))
+    summed = lax.psum(lax.psum(gram_terms(spectra), "py"), "px")
     total_points = point_count * lax.axis_size("px") * lax.axis_size("py")
     gram = summed / jnp.float32(total_points * VARS)
     return (spectra, gram)

time: 308 us -> 305 us (level)
    psum x1 -> x2, blocking collectives: 17.6 us -> 14.7 us  [on_device(): summed = lax.psum(lax.psum(gram_terms(spectra), 'py'), 'px')]
where the time goes in v1:
time: 305 us; the launch traced here: 304 us
  waiting for transfers between devices  189 us (62%)
  matrix products  39.8 us (13%)
  local copies, waits for them, and re-layouts  37.3 us (12%)
  blocking collectives  14.7 us (5%)
  between operations  14.1 us (5%)
  other arithmetic  8.88 us (3%)
    reduce_scatter x1, waiting for transfers between devices, on_device(): lax.psum_scatter(jnp.dot(rotation_multipliers, flat_snapshots, preferred_...  189 us
    dot_general x1, matrix products, gram_terms(): jnp.einsum('fam,fbm->fab', flat, flat, precision=lax.Precision.HIGHEST)  25.9 us
    unnamed x5, local copies, waits for them, and re-layouts  23.9 us
    psum x2, blocking collectives, on_device(): summed = lax.psum(lax.psum(gram_terms(spectra), 'py'), 'px')  14.7 us
    dot_general x1, matrix products, on_device(): jnp.dot(rotation_multipliers, flat_snapshots, preferred_element_type=jnp....  13.8 us
    reshape x2, local copies, waits for them, and re-layouts, on_device(): raw.reshape(RETAINED_MODES // groups, SEGMENT_NUMBER, 2, VARS, point_count)  13.2 us
    mul x1, other arithmetic, on_device(): spectra = raw * jnp.sqrt(quad_weights)  7.77 us
  transfers between devices with their start and end apart: 1, of which 1 were waited for; matrix products, arithmetic and copies ran while one was open for 0% of the time, Pallas kernels for 0%

profile of v1, /device:TPU:1, one launch (start us, length us, event | category | flops | bytes accessed | tf_op | source)
XLA Modules:
  0.0 303.7 jit_solution(4045065501944685693)
XLA Ops:
  7.2 0.0 reduce-scatter.2.cloned.1.call-start
  7.2 0.1 broadcast_subtract_fusion
  7.3 0.1 fusion.6
  7.4 0.9 multiply_convert_fusion.1
  8.4 12.7 %copy.17 = bf16[96,5,8192]{0,2,1:T(8,128)(2,1)} copy(bf16[96,5,8192]{2,0,1:T(8,128)(2,1)} %param.3) | data formatting | bytes 15728640 | tf_op args[0]
  21.1 13.8 %fusion.7 = f32[128,40960]{1,0:T(8,128)} fusion(bf16[128,96]{1,0:T(8,128)(2,1)S(1)} %bitcast.8, bf16[96,40960]{0,1:T(8,128)(2,1)} %bitcast.7), kind=kOutput, calls=%fused_computation.24 | convolution fusion | flops 1006632960 | bytes 28860416 | tf_op jit(solution)/shard_map/dot_general | solution.py:49
  34.9 0.0 copy-start
  34.9 0.0 reduce-scatter.2.cloned.1.call-update
  34.9 0.7 copy-done
  35.7 0.1 mul.103
  35.8 188.9 %reduce-scatter.2.cloned.1.call-done = f32[32,40960]{1,0:T(8,128)} async-done(((f32[128,40960]{1,0:T(8,128)}), f32[32,40960]{1,0:T(8,128)}) %reduce-scatter.2.cloned.1.call-update) | async-done | bytes 5242896 | tf_op jit(solution)/shard_map/reduce_scatter | solution.py:48
  224.7 5.8 %reshape.194 = f32[8,4,40960]{2,1,0:T(4,128)} reshape(f32[32,40960]{1,0:T(8,128)} %reduce-scatter.2.cloned.1.call-done) | data formatting | bytes 10485760 | tf_op jit(solution)/shard_map/reshape | solution.py:54
  230.6 25.9 %fusion = f32[8,4,4]{2,1,0:T(4,128)S(1)} fusion(f32[8,4,40960]{2,1,0:T(4,128)} %reshape.194, f32[40960]{0:T(1024)S(1)} %mul.103), kind=kOutput, calls=%fused_computation | convolution fusion | flops 64225280 | bytes 5407232 | tf_op jit(solution)/shard_map/fam,fbm->fab/dot_general | solution.py:32
  256.5 0.1 copy.18
  256.7 9.7 %psum.14 = f32[8,2,2,2]{0,2,3,1:T(2,128)S(1)} all-reduce(f32[8,2,2,2]{0,2,3,1:T(2,128)S(1)} %pad_maximum_fusion.1), channel_id=1, replica_groups=mesh['px'=2,'py'=4,'ta'=4] {'py'}, use_global_device_ids=true, to_apply=%region_1.2 | all-reduce | flops 64 | bytes 512 | tf_op jit(solution)/shard_map/psum | solution.py:56
  266.3 5.0 %psum.15 = f32[8,2,2,2]{0,2,3,1:T(2,128)S(1)} all-reduce(f32[8,2,2,2]{0,2,3,1:T(2,128)S(1)} %psum.14), channel_id=1, replica_groups=mesh['px'=2,'py'=4,'ta'=4] {'px'}, use_global_device_ids=true, to_apply=%region_2.3 | all-reduce | flops 64 | bytes 512 | tf_op jit(solution)/shard_map/psum | solution.py:56
  271.3 0.6 copy.20
  271.9 7.3 %reshape.193 = f32[8,2,2,5,8192]{4,3,2,1,0:T(8,128)} reshape(f32[32,40960]{1,0:T(8,128)} %reduce-scatter.2.cloned.1.call-done) | data formatting | bytes 10485760 | tf_op jit(solution)/shard_map/reshape | solution.py:54
  279.3 7.8 %broadcast_multiply_fusion = f32[8,2,2,5,8192]{4,3,2,1,0:T(8,128)} fusion(f32[8,2,2,5,8192]{4,3,2,1,0:T(8,128)} %reshape.193, f32[8192]{0:T(1024)S(1)} %sqrt.3), kind=kLoop, calls=%fused_computation.2 | loop fusion | flops 1310720 | bytes 10518528 | tf_op jit(solution)/shard_map/mul | solution.py:55
  287.0 9.8 %copy.19 = f32[8,2,2,5,8192]{4,2,3,1,0:T(2,128)} copy(f32[8,2,2,5,8192]{4,3,2,1,0:T(8,128)} %broadcast_multiply_fusion) | data formatting | bytes 10485760
  (9 shorter events, 0.1 us)
Async XLA Ops:
  7.2 217.6 %reduce-scatter.2.cloned.1.call-start = ((), (), s32[]{:S(2)}) async-start(), calls=%async_computation.1 | async-start | bytes 26214400 | tf_op jit(solution)/shard_map/reduce_scatter | solution.py:48
  34.9 0.8 copy-start
Sparse Core Ops, SparseCore 0:
  35.1 189.6 reduce-scatter.1
